TPU v7x, 32 devices: a whole 2x2x4 slice. The times are simulated.
32 devices in a mesh: seq: 8 (over y, x, core), sub: 4 (over z).
Axes of the slice: x: 2, y: 2, z: 4, core: 2. Of those that a mesh axis runs over, the one named last changes fastest.
Arguments:
- tokens: bfloat16 [2048, 4096], P('seq'), may hold values from -6 to 6
- w_split: bfloat16 [4096, 4096], P(None, 'sub'), may hold values from -0.09375 to 0.09375
- w_merge: bfloat16 [4096, 4096], P('sub'), may hold values from -0.09375 to 0.09375
- expert_in: bfloat16 [32, 1024, 2048], P(('seq', 'sub')), may hold values from -0.1875 to 0.1875
- expert_out: bfloat16 [32, 1024, 1024], P(('seq', 'sub')), may hold values from -0.1875 to 0.1875
- expert_ids: int32 [4, 2048, 2], P('sub', 'seq'), may hold values from 0 to 31, all different within a row; in each aligned block of 256 rows (0 to 255, 256 to 511, ..., all dimensions but the last counted through in order) at most 24 rows name the same one
- combine_q: int32 [4, 2048, 2], P('sub', 'seq'), may hold values from 4096 to 65536
- capacity: int32 [32], replicated, may hold values from 12 to 24
Outputs:
- mixed: bfloat16 [2048, 4096], P('seq', 'sub')
Inputs may be any that keep to these rules, and one draw needn't show every extreme that they name: `expert_ids`: in each block of 256 positions of one sub-head, the ids of a position differ, no expert is named more than 24 times, a bound that some block reaches.
All inputs are finite; a program needn't handle non-finite values.
Results may differ from a plain program's by a relative error of at most 0.0076.
Values may be sent and summed in bfloat16 or wider, within the bound.
A program may use at most 128 MiB of HBM per device.

v0:
```python
import functools

import jax
import jax.numpy as jnp
from jax import lax
from jax.experimental import pallas as pl
from jax.experimental.pallas import tpu as pltpu
from jax.sharding import PartitionSpec as P

MESH = pl.DeviceIdType.MESH
GROUPS = 4
TILE = 256
CHUNKS = 2
EXPERTS_VMEM = 28 * 1024 * 1024
MERGE_VMEM = 28 * 1024 * 1024


def experts_kernel(n_seq, n_sub, slots, sub_tok, ids, quanta, capacity, w_in_hbm, w_out_hbm, head,
                   packed, received, answers, returned, hidden, w_in, w_out, w_sem,
                   send_sem, recv_sem, back_sem, ret_sem):
    n = n_seq * n_sub
    me = lax.axis_index("seq") * n_sub + lax.axis_index("sub")
    tok_rows, width = sub_tok.shape
    half = width // 2
    block = 2 * slots
    per = n // GROUPS
    ffe = w_out.shape[0]

    fetch_in = pltpu.make_async_copy(w_in_hbm, w_in, w_sem.at[0])
    fetch_out = pltpu.make_async_copy(w_out_hbm, w_out, w_sem.at[1])

    def rows(i):
        return pl.ds(pl.multiple_of(i * block, 16), block)

    def span(g):
        return pl.ds(pl.multiple_of(g * per * block, 16), per * block)

    def device(i):
        return (i // n_sub, lax.rem(i, n_sub))

    def outgoing(i):
        return pltpu.make_async_remote_copy(
            src_ref=packed.at[rows(i)], dst_ref=received.at[rows(i)],
            send_sem=send_sem.at[i], recv_sem=recv_sem.at[i],
            device_id=device(lax.rem(me + i, n)), device_id_type=MESH)

    def homeward(i):
        return pltpu.make_async_remote_copy(
            src_ref=answers.at[rows(i)], dst_ref=returned.at[rows(i)],
            send_sem=back_sem.at[i], recv_sem=ret_sem.at[i],
            device_id=device(lax.rem(me + n - i, n)), device_id_type=MESH)

    def fold(y):
        y = y.reshape(per, slots, width)
        y = jnp.concatenate([y[:, :, :half], y[:, :, half:]], axis=1)
        return y.reshape(per * block, half).astype(jnp.bfloat16)

    def unfold(x):
        x = x.astype(jnp.float32).reshape(per, block, half)
        return jnp.concatenate(
            [x[:, :slots].reshape(per * slots, half), x[:, slots:].reshape(per * slots, half)],
            axis=1).astype(jnp.bfloat16)

    places = lax.broadcasted_iota(jnp.int32, (n, tok_rows), 0)
    named = [(places == ids[k:k + 1, :]).astype(jnp.float32) for k in range(2)]
    before = (lax.broadcasted_iota(jnp.int32, (tok_rows, tok_rows), 0)
              < lax.broadcasted_iota(jnp.int32, (tok_rows, tok_rows), 1))
    earlier = jnp.dot((named[0] + named[1]).astype(jnp.bfloat16),
                      before.astype(jnp.float32).astype(jnp.bfloat16),
                      preferred_element_type=jnp.float32)
    square = lax.broadcasted_iota(jnp.int32, (n, n), 0)
    across = lax.broadcasted_iota(jnp.int32, (n, n), 1)
    limit = jnp.sum(jnp.where(square == across, capacity[...].astype(jnp.float32), 0.0),
                    axis=1, keepdims=True)
    slot, weight = [], []
    for k in range(2):
        rank = jnp.sum(named[k] * earlier, axis=0, keepdims=True)
        most = jnp.sum(named[k] * limit, axis=0, keepdims=True)
        away = ids[k:k + 1, :] - me
        away = jnp.where(away < 0, away + n, away)
        slot.append(jnp.where(rank < most, away * slots + rank.astype(jnp.int32), -1))
        weight.append(quanta[k:k + 1, :].astype(jnp.float32) / 65536.0)

    def spread(g, values):
        at = lax.broadcasted_iota(jnp.int32, (per * slots, tok_rows), 0) + g * (per * slots)
        return (jnp.where(at == slot[0], values[0], 0.0)
                + jnp.where(at == slot[1], values[1], 0.0))

    for g in range(GROUPS):
        chosen = spread(g, (1.0, 1.0)).astype(jnp.bfloat16)
        packed[span(g), :] = fold(jnp.dot(chosen, sub_tok[...],
                                          preferred_element_type=jnp.float32))

        @pl.loop(max(1, g * per), (g + 1) * per)
        def _(i):
            outgoing(i).start()

        if g == 0:
            fetch_in.start()
            fetch_out.start()

    received[0:block, :] = packed[0:block, :]
    fetch_in.wait()
    fetch_out.wait()

    @pl.loop(0, GROUPS)
    def _(g):
        first = g * per
        low = jnp.where(g == 0, 1, first)

        @pl.loop(low, first + per)
        def _(i):
            outgoing(i).wait_recv()

        x = unfold(received[span(g), :])

        @pl.loop(0, ffe // TILE)
        def _(c):
            gate_at = pl.ds(pl.multiple_of(c * TILE, TILE), TILE)
            up_at = pl.ds(pl.multiple_of(ffe + c * TILE, TILE), TILE)
            gate = jnp.dot(x, w_in[:, gate_at], preferred_element_type=jnp.float32)
            up = jnp.dot(x, w_in[:, up_at], preferred_element_type=jnp.float32)
            hidden[:, gate_at] = (gate / (1.0 + jnp.exp(-gate)) * up).astype(jnp.bfloat16)

        act = hidden[...]
        parts = []
        for h in range(2):
            y = jnp.dot(act, w_out[:, h * half:(h + 1) * half],
                        preferred_element_type=jnp.float32)
            parts.append(y.reshape(per, slots, half))
        y = jnp.concatenate(parts, axis=1).reshape(per * block, half)
        answers[span(g), :] = y.astype(jnp.bfloat16)

        @pl.loop(low, first + per)
        def _(i):
            homeward(i).start()

    returned[0:block, :] = answers[0:block, :]
    summed = jnp.zeros((tok_rows, width), jnp.float32)
    for g in range(GROUPS):
        @pl.loop(max(1, g * per), (g + 1) * per)
        def _(i):
            homeward(i).wait_recv()

        full = spread(g, weight)
        high = full.astype(jnp.bfloat16)
        low = (full - high.astype(jnp.float32)).astype(jnp.bfloat16)
        y = unfold(returned[span(g), :])
        for part in (high, low):
            summed = summed + lax.dot_general(part, y, (((0,), (0,)), ((), ())),
                                              preferred_element_type=jnp.float32)
    head[...] = summed.astype(jnp.bfloat16)

    @pl.loop(1, n)
    def _(i):
        outgoing(i).wait_send()
        homeward(i).wait_send()


def exchange_experts(n_seq, n_sub, slots, sub_tok, ids, quanta, capacity, w_in, w_out):
    n = n_seq * n_sub
    width = w_out.shape[1]
    vmem = pl.BlockSpec(memory_space=pltpu.VMEM)
    hbm = pl.BlockSpec(memory_space=pltpu.HBM)
    rows = n * slots // GROUPS
    crossing = pltpu.VMEM((n * 2 * slots, width // 2), jnp.bfloat16)
    return pl.pallas_call(
        functools.partial(experts_kernel, n_seq, n_sub, slots),
        out_shape=jax.ShapeDtypeStruct(sub_tok.shape, jnp.bfloat16),
        in_specs=[vmem] * 4 + [hbm] * 2,
        out_specs=vmem,
        scratch_shapes=[crossing] * 4 + [
            pltpu.VMEM((rows, w_out.shape[0]), jnp.bfloat16),
            pltpu.VMEM(w_in.shape, jnp.bfloat16),
            pltpu.VMEM(w_out.shape, jnp.bfloat16),
            pltpu.SemaphoreType.DMA((2,)),
        ] + [pltpu.SemaphoreType.DMA((n,))] * 4,
        compiler_params=pltpu.CompilerParams(
            has_side_effects=True, vmem_limit_bytes=EXPERTS_VMEM),
        name="experts",
    )(sub_tok, ids, quanta, capacity, w_in, w_out)


def merge_kernel(n, head, w, out, total, sending, landed, send_sem, recv_sem):
    z = lax.axis_index("sub")
    rows, width = out.shape
    piece = rows // CHUNKS

    def target(j):
        near_low = jnp.where(j < n - 1 - z, n - 1 - j, j - (n - 1 - z))
        near_high = jnp.where(j < z, j, n - 1 - (j - z))
        return jnp.where(z < n // 2, near_low, near_high)

    barrier = pltpu.get_barrier_semaphore()

    @pl.when(z > 0)
    def _():
        pl.semaphore_signal(barrier, inc=1, device_id={"sub": z - 1}, device_id_type=MESH)

    @pl.when(z < n - 1)
    def _():
        pl.semaphore_signal(barrier, inc=1, device_id={"sub": z + 1}, device_id_type=MESH)

    pl.semaphore_wait(barrier, jnp.where(z > 0, 1, 0) + jnp.where(z < n - 1, 1, 0))

    def hop(way, t, c):
        part = pl.ds(c * piece, piece)
        return pltpu.make_async_remote_copy(
            src_ref=sending.at[t, part], dst_ref=landed.at[way, t, part],
            send_sem=send_sem.at[t, c], recv_sem=recv_sem.at[way, t, c],
            device_id={"sub": z + (1 if way == 0 else -1)}, device_id_type=MESH)

    for j in range(n):
        t = target(j)
        steps = 2 if j == 0 else 1
        for step in range(steps):
            tall = pl.ds(step * (rows // steps), rows // steps)

            @pl.loop(0, width // TILE)
            def _(k):
                cols = pl.ds(pl.multiple_of(k * TILE, TILE), TILE)
                from_cols = pl.ds(pl.multiple_of(t * width + k * TILE, TILE), TILE)
                total[t, tall, cols] = jnp.dot(head[tall, :], w[:, from_cols],
                                               preferred_element_type=jnp.float32)

            for way, source in ((0, 0), (1, n - 1)):
                @pl.when((z == source) & (t != z))
                def _():
                    for c in range(step * CHUNKS // steps, (step + 1) * CHUNKS // steps):
                        part = pl.ds(c * piece, piece)
                        sending[t, part, :] = total[t, part, :].astype(jnp.bfloat16)
                        hop(way, t, c).start()

    def relay(way, when):
        for k in range(n - 2):
            t = n - 1 - k if way == 0 else k
            inside = (z > 0) & (z < t) if way == 0 else (z < n - 1) & (z > t)

            @pl.when(inside & when)
            def _():
                for c in range(CHUNKS):
                    part = pl.ds(c * piece, piece)
                    hop(way, t, c).wait_recv()
                    sending[t, part, :] = (
                        total[t, part, :] + landed[way, t, part, :].astype(jnp.float32)
                    ).astype(jnp.bfloat16)
                    hop(way, t, c).start()

    relay(0, z < n // 2)
    relay(1, z >= 0)
    relay(0, z >= n // 2)

    for way, has in ((0, z > 0), (1, z < n - 1)):
        @pl.when(has)
        def _():
            for c in range(CHUNKS):
                part = pl.ds(c * piece, piece)
                hop(way, z, c).wait_recv()
                total[z, part, :] += landed[way, z, part, :].astype(jnp.float32)

    out[...] = total[z].astype(out.dtype)
    for t in range(n):
        @pl.when(z < t)
        def _():
            for c in range(CHUNKS):
                hop(0, t, c).wait_send()

        @pl.when(z > t)
        def _():
            for c in range(CHUNKS):
                hop(1, t, c).wait_send()


def merge_scatter(n, head, w_merge):
    rows, width = head.shape[0], w_merge.shape[1] // n
    vmem = pl.BlockSpec(memory_space=pltpu.VMEM)
    return pl.pallas_call(
        functools.partial(merge_kernel, n),
        out_shape=jax.ShapeDtypeStruct((rows, width), jnp.bfloat16),
        in_specs=[vmem, vmem],
        out_specs=vmem,
        scratch_shapes=[
            pltpu.VMEM((n, rows, width), jnp.float32),
            pltpu.VMEM((n, rows, width), jnp.bfloat16),
            pltpu.VMEM((2, n, rows, width), jnp.bfloat16),
            pltpu.SemaphoreType.DMA((n, CHUNKS)),
            pltpu.SemaphoreType.DMA((2, n, CHUNKS)),
        ],
        compiler_params=pltpu.CompilerParams(
            collective_id=1, has_side_effects=True, vmem_limit_bytes=MERGE_VMEM),
        name="merge",
    )(head, w_merge)


def body(n_seq, n_sub, tokens, w_split, w_merge, expert_in, expert_out, expert_ids, combine_q,
         capacity):
    sub_tok = jnp.dot(tokens, w_split, preferred_element_type=jnp.float32).astype(jnp.bfloat16)
    sub_tok, w_merge = lax.optimization_barrier((sub_tok, w_merge))
    tok_rows = tokens.shape[0]
    experts = capacity.shape[0]
    slot_count = -(-(3 * tok_rows // experts) // 8) * 8
    head_out = exchange_experts(
        n_seq, n_sub, slot_count, sub_tok, expert_ids[0].T, combine_q[0].T, capacity[None, :],
        expert_in[0], expert_out[0])
    return merge_scatter(n_sub, head_out, w_merge)


def solution(mesh):
    in_specs = (
        P("seq", None),
        P(None, "sub"),
        P("sub", None),
        P(("seq", "sub"), None, None),
        P(("seq", "sub"), None, None),
        P("sub", "seq", None),
        P("sub", "seq", None),
        P(),
    )
    out_specs = P("seq", "sub")
    call = functools.partial(body, mesh.shape["seq"], mesh.shape["sub"])
    return jax.shard_map(call, mesh=mesh, in_specs=in_specs, out_specs=out_specs, check_vma=False)
```

profile of v0, /device:TPU:0, one launch (start us, length us, event | category | flops | bytes accessed | tf_op | source)
XLA Modules:
  0.0 126.4 jit_solution(1604765754997439813)
XLA Ops:
  0.0 0.0 copy-start
  0.0 1.6 %copy-done = bf16[256,4096]{1,0:T(8,128)(2,1)S(1)} copy-done((bf16[256,4096]{1,0:T(8,128)(2,1)S(1)}, bf16[256,4096]{1,0:T(8,128)(2,1)}, u32[]{:S(2)}) %copy-start) | copy-done | bytes 2097176
  1.6 0.0 copy-start.2
  1.6 0.0 copy-start.3
  1.6 0.0 copy-start.4
  1.6 0.0 copy-start.5
  1.6 0.0 copy-start.6
  1.6 0.0 copy-start.1
  1.6 5.9 %convolution_convert_fusion.sub_tok = bf16[256,1024]{1,0:T(8,128)(2,1)S(1)} fusion(bf16[256,4096]{1,0:T(8,128)(2,1)S(1)} %copy-done, bf16[4096,1024]{1,0:T(8,128)(2,1)} %param.9), kind=kOutput, calls=%fused_computation | convolution fusion | flops 2147745792 | bytes 11010048 | tf_op jit(solution)/shard_map/dot_general | solution.py:297
  7.5 0.0 copy-done.2
  7.5 0.0 copy-done.3
  7.5 0.0 copy-done.4
  7.5 0.0 copy-done.5
  7.5 0.0 copy-done.6
  7.5 81.9 %experts.1.head = bf16[256,1024]{1,0:T(8,128)(2,1)S(1)} custom-call(bf16[256,1024]{1,0:T(8,128)(2,1)S(1)} %convolution_convert_fusion.sub_tok, s32[2,256]{1,0:T(2,128)S(1)} %bitcast.13, s32[2,256]{1,0:T(2,128)S(1)} %bitcast.14, s32[1,32]{1,0:T(1,128)S(1)} %bitcast.15, bf16[1024,2048]{1,0:T(8,128)(2,1)S(1)} %bitcast.11, bf16[1024,1024]{1,0:T(8,128)(2,1)S(1)} %bitcast.12), custom_call_target="tpu_custom_call" | custom-call | tf_op jit(solution)/shard_map/experts/pallas_call | solution.py:167
  89.5 0.0 copy-done.1
  89.5 36.1 %merge.1 = bf16[256,1024]{1,0:T(8,128)(2,1)S(1)} custom-call(bf16[256,1024]{1,0:T(8,128)(2,1)S(1)} %experts.1.head, bf16[1024,4096]{1,0:T(8,128)(2,1)S(1)} %copy-done.1), custom_call_target="tpu_custom_call" | custom-call | tf_op jit(solution)/shard_map/merge/pallas_call | solution.py:277
  125.6 0.8 copy.10
Async XLA Ops:
  0.0 1.6 %copy-start = (bf16[256,4096]{1,0:T(8,128)(2,1)S(1)}, bf16[256,4096]{1,0:T(8,128)(2,1)}, u32[]{:S(2)}) copy-start(bf16[256,4096]{1,0:T(8,128)(2,1)} %param.8) | copy-start | bytes 6291460
  1.6 5.9 %copy-start.2 = (bf16[1,1024,2048]{2,1,0:T(8,128)(2,1)S(1)}, bf16[1,1024,2048]{2,1,0:T(8,128)(2,1)}, u32[]{:S(2)}) copy-start(bf16[1,1024,2048]{2,1,0:T(8,128)(2,1)} %param.11) | copy-start | bytes 12582916
  1.6 5.9 %copy-start.3 = (bf16[1,1024,1024]{2,1,0:T(8,128)(2,1)S(1)}, bf16[1,1024,1024]{2,1,0:T(8,128)(2,1)}, u32[]{:S(2)}) copy-start(bf16[1,1024,1024]{2,1,0:T(8,128)(2,1)} %param.12) | copy-start | bytes 6291460
  1.6 5.9 %copy-start.4 = (s32[1,256,2]{1,2,0:T(2,128)S(1)}, s32[1,256,2]{1,2,0:T(2,128)}, u32[]{:S(2)}) copy-start(s32[1,256,2]{1,2,0:T(2,128)} %param.13) | copy-start | bytes 6148
  1.6 5.9 %copy-start.5 = (s32[1,256,2]{1,2,0:T(2,128)S(1)}, s32[1,256,2]{1,2,0:T(2,128)}, u32[]{:S(2)}) copy-start(s32[1,256,2]{1,2,0:T(2,128)} %param.14) | copy-start | bytes 6148
  1.6 5.9 %copy-start.6 = (s32[32]{0:T(128)S(1)}, s32[32]{0:T(128)}, u32[]{:S(2)}) copy-start(s32[32]{0:T(128)} %param.15) | copy-start | bytes 388
  1.6 87.9 %copy-start.1 = (bf16[1024,4096]{1,0:T(8,128)(2,1)S(1)}, bf16[1024,4096]{1,0:T(8,128)(2,1)}, u32[]{:S(2)}) copy-start(bf16[1024,4096]{1,0:T(8,128)(2,1)} %w) | copy-start | bytes 25165828
where the time goes:
time: 127 us; the launch traced here: 126 us
  Pallas kernels  118 us (93%)
  matrix products  5.86 us (5%)
  local copies, waits for them, and re-layouts  2.41 us (2%)
    pallas_call x1, Pallas kernels, exchange_experts(): pl.pallas_call(functools.partial(experts_kernel, n_seq, n_sub, slots), ou...  81.9 us
    pallas_call x1, Pallas kernels, merge_scatter(): pl.pallas_call(functools.partial(merge_kernel, n), out_shape=jax.ShapeDty...  36.1 us
    dot_general x1, matrix products, body(): jnp.dot(tokens, w_split, preferred_element_type=jnp.float32)  5.86 us

commit v1 on v0

v1 whole, which is shorter than its diff:
```python
import functools

import jax
import jax.numpy as jnp
from jax import lax
from jax.experimental import pallas as pl
from jax.experimental.pallas import tpu as pltpu
from jax.sharding import PartitionSpec as P

MESH = pl.DeviceIdType.MESH
TILE = 256
CHUNKS = 4
LAG = 2
VMEM_BYTES = 60 * 1024 * 1024
F32 = jnp.float32
BF16 = jnp.bfloat16


def layer_kernel(n_seq, n_sub, slots, route, capacity, tokens_hbm, w_split_hbm, w_in_hbm,
                 w_out_hbm, w_merge_hbm, out,
                 tokens, w_split, w_in, w_out, w_merge, info, mine, raw, pick, mix, packed,
                 received, x, hidden, answers, returned, part_out, part_in, acc, head,
                 sending, landed,
                 load_sem, info_send, info_recv, raw_send, raw_recv, slot_send, slot_recv,
                 ans_send, ans_recv, part_send, part_recv, hop_send, hop_recv):
    s, z = lax.axis_index("seq"), lax.axis_index("sub")
    half = n_sub // 2
    side = z // half
    q = jnp.where(side == 0, z, n_sub - 1 - z)
    inner = q == half - 1
    n = n_seq * n_sub
    peers = half * n_seq
    rows, width = acc.shape
    wide = width // CHUNKS
    fold_w = wide // 2
    ffe = w_out.shape[0]
    group = n_seq * slots

    def plane(where, depth):
        return jnp.where(where == 0, depth, n_sub - 1 - depth)

    def near(r, depth):
        return (lax.rem(s + r, n_seq), plane(side, depth))

    def across(depth):
        return (s, plane(1 - side, depth))

    fetch_tokens = pltpu.make_async_copy(tokens_hbm, tokens, load_sem.at[CHUNKS])
    fetch_in = pltpu.make_async_copy(w_in_hbm, w_in, load_sem.at[CHUNKS + 1])
    fetch_out = pltpu.make_async_copy(w_out_hbm, w_out, load_sem.at[CHUNKS + 2])
    fetch_merge = pltpu.make_async_copy(w_merge_hbm, w_merge, load_sem.at[CHUNKS + 3])

    def fetch_split(c):
        return pltpu.make_async_copy(
            w_split_hbm.at[:, pl.ds(c * wide, wide)], w_split.at[c], load_sem.at[c])

    fetch_tokens.start()
    for c in range(CHUNKS):
        fetch_split(c).start()

    barrier = pltpu.get_barrier_semaphore()
    for p in range(half):
        @pl.loop(0, n_seq)
        def _(r):
            @pl.when((r != 0) | (q != p))
            def _():
                pl.semaphore_signal(barrier, inc=1, device_id=near(r, p), device_id_type=MESH)

        @pl.when(inner | (p == half - 1))
        def _():
            pl.semaphore_signal(barrier, inc=1, device_id=across(p), device_id_type=MESH)

    def remote(src, dst, send, recv, to):
        return pltpu.make_async_remote_copy(src_ref=src, dst_ref=dst, send_sem=send,
                                            recv_sem=recv, device_id=to, device_id_type=MESH)

    def info_copy():
        return remote(route, info.at[q], info_send.at[0], info_recv.at[q], across(half - 1))

    def raw_copy(c):
        return remote(mine.at[c], raw.at[q, c], raw_send.at[c], raw_recv.at[q, c],
                      across(half - 1))

    def part_copy(j, c):
        return remote(part_out.at[j, c], part_in.at[c], part_send.at[j, c], part_recv.at[c],
                      across(j))

    def whole(ref, sem):
        return pltpu.make_async_copy(ref, ref, sem)

    def ship(b, g, c):
        for p in range(half):
            @pl.loop(0, n_seq)
            def _(r):
                @pl.when((r != 0) | (q != p))
                def _():
                    remote(packed.at[b, c, p * n_seq + r], received.at[g, c, r],
                           slot_send.at[b, c], slot_recv.at[g, c], near(r, p)).start()

        received[g, c, 0:1] = packed[b, c, pl.ds(q * n_seq, 1)]

    def seat_here(g):
        return jnp.minimum(g, half - 1) == q

    def fold(y, count):
        y = y.reshape(count, slots, wide)
        return jnp.concatenate([y[:, :, :fold_w], y[:, :, fold_w:]], axis=1).astype(BF16)

    def unfold(y, count):
        y = y.astype(F32)
        return (y[:, :slots].reshape(count * slots, fold_w).astype(BF16),
                y[:, slots:].reshape(count * slots, fold_w).astype(BF16))

    def pack(b, block, c):
        y = jnp.dot(pick[b], block, preferred_element_type=F32)
        packed[b, c] = fold(y, peers)

    square = lax.broadcasted_iota(jnp.int32, (n, n), 0)
    cross = lax.broadcasted_iota(jnp.int32, (n, n), 1)
    limit = jnp.sum(jnp.where(square == cross, capacity[...].astype(F32), 0.0),
                    axis=1, keepdims=True)
    expert = lax.broadcasted_iota(jnp.int32, (n, 1), 0).astype(F32)
    expert_seq = jnp.floor((expert + 0.5) / n_sub)
    expert_sub = (expert - expert_seq * n_sub).astype(jnp.int32)
    away = expert_seq.astype(jnp.int32) - s
    away = jnp.where(away < 0, away + n_seq, away)
    depth = jnp.where(side == 0, expert_sub, n_sub - 1 - expert_sub)
    seats = jnp.where(depth < half, (depth * n_seq + away) * slots, -1).astype(F32)

    def tables(ids, b):
        places = lax.broadcasted_iota(jnp.int32, (n, rows), 0)
        named = [(places == ids[k:k + 1, :]).astype(F32) for k in range(2)]
        before = (lax.broadcasted_iota(jnp.int32, (rows, rows), 0)
                  < lax.broadcasted_iota(jnp.int32, (rows, rows), 1))
        earlier = jnp.dot((named[0] + named[1]).astype(BF16), before.astype(F32).astype(BF16),
                          preferred_element_type=F32)
        slot, weight = [], []
        for k in range(2):
            rank = jnp.sum(named[k] * earlier, axis=0, keepdims=True)
            most = jnp.sum(named[k] * limit, axis=0, keepdims=True)
            seat = jnp.sum(named[k] * seats, axis=0, keepdims=True)
            kept = (rank < most) & (seat >= 0.0)
            slot.append(jnp.where(kept, seat + rank, -1.0).astype(jnp.int32))
            weight.append(ids[2 + k:3 + k, :].astype(F32) / 65536.0)
        at = lax.broadcasted_iota(jnp.int32, (peers * slots, rows), 0)
        first, second = at == slot[0], at == slot[1]
        pick[b] = (jnp.where(first, 1.0, 0.0) + jnp.where(second, 1.0, 0.0)).astype(BF16)
        full = jnp.where(first, weight[0], 0.0) + jnp.where(second, weight[1], 0.0)
        mix[b] = full.T.astype(BF16)

    tables(route[...], 0)

    fetch_tokens.wait()
    for c in range(CHUNKS):
        fetch_split(c).wait()
        for k in range(0, wide, TILE):
            mine[c, :, k:k + TILE] = jnp.dot(
                tokens[...], w_split[c, :, k:k + TILE], preferred_element_type=F32).astype(BF16)
        if c == 0:
            fetch_in.start()
            fetch_out.start()
            pl.semaphore_wait(barrier, peers - 1 + jnp.where(inner, half, 1))
            info_copy().start()

        @pl.when(~inner | (half == 1))
        def _():
            raw_copy(c).start()

        pack(0, mine[c], c)
        ship(0, q, c)

    fetch_merge.start()

    @pl.when(inner)
    def _():
        @pl.loop(0, half)
        def _(j):
            whole(info.at[j], info_recv.at[j]).wait()
            tables(info[j], 1 + j)

    def proxy(j, first, last):
        @pl.when(inner)
        def _():
            for c in range(first, last):
                whole(raw.at[j, c], raw_recv.at[j, c]).wait()
                pack(1 + j, raw[j, c], c)
                ship(1 + j, half + j, c)
                if j == 0 and half > 1:
                    for own in range(CHUNKS):
                        if min(own + LAG, CHUNKS - 1) == c:
                            raw_copy(own).start()

    def ffn(g):
        for c in range(CHUNKS):
            @pl.when(seat_here(g))
            def _():
                whole(received.at[g, c, pl.ds(0, n_seq - 1)], slot_recv.at[g, c]).wait()

            @pl.when(~seat_here(g))
            def _():
                whole(received.at[g, c], slot_recv.at[g, c]).wait()

            left, right = unfold(received[g, c], n_seq)
            x[:, c * wide:c * wide + fold_w] = left
            x[:, c * wide + fold_w:(c + 1) * wide] = right

        @pl.loop(0, ffe // TILE)
        def _(t):
            gate_at = pl.ds(pl.multiple_of(t * TILE, TILE), TILE)
            up_at = pl.ds(pl.multiple_of(ffe + t * TILE, TILE), TILE)
            gate = jnp.dot(x[...], w_in[:, gate_at], preferred_element_type=F32)
            up = jnp.dot(x[...], w_in[:, up_at], preferred_element_type=F32)
            hidden[:, gate_at] = (gate / (1.0 + jnp.exp(-gate)) * up).astype(BF16)

        to = jnp.minimum(g, half - 1)
        b = jnp.maximum(g - half + 1, 0)
        for c in range(CHUNKS):
            y = jnp.dot(hidden[...], w_out[:, c * wide:(c + 1) * wide],
                        preferred_element_type=F32)
            answers[g, c] = fold(y, n_seq)

            @pl.loop(0, n_seq)
            def _(r):
                @pl.when((r != 0) | (q != to))
                def _():
                    remote(answers.at[g, c, r], returned.at[b, c, q * n_seq + r],
                           ans_send.at[g, c], ans_recv.at[b, c],
                           near(n_seq - r, to)).start()

            @pl.when(q == to)
            def _():
                returned[b, c, pl.ds(q * n_seq, 1)] = answers[g, c, 0:1]

    def combine(b, c):
        whole(returned.at[b, c, pl.ds(0, peers - 1)], ans_recv.at[b, c]).wait()
        left, right = unfold(returned[b, c], peers)
        return jnp.dot(mix[b], jnp.concatenate([left, right], axis=1),
                       preferred_element_type=F32)

    def bring_back(j):
        @pl.when(inner)
        def _():
            for c in range(CHUNKS):
                part_out[j, c] = combine(1 + j, c).astype(BF16)
                part_copy(j, c).start()

    fetch_in.wait()
    fetch_out.wait()
    middle = CHUNKS // 2
    proxy(0, 0, middle)
    ffn(q)
    proxy(0, middle, CHUNKS)
    for i in range(1, half):
        ffn(lax.rem(q + i, half))
    for j in range(half):
        last = j == half - 1
        if j > 0:
            proxy(j, 0, CHUNKS)
        if last:
            for c in range(CHUNKS):
                acc[:, c * wide:(c + 1) * wide] = combine(0, c)
            for k in range(half - 1):
                bring_back(k)
        ffn(half + j)
    bring_back(half - 1)

    for c in range(CHUNKS):
        at = slice(c * wide, (c + 1) * wide)
        whole(part_in.at[c], part_recv.at[c]).wait()
        head[:, at] = (acc[:, at] + part_in[c].astype(F32)).astype(BF16)

    fetch_merge.wait()
    tiles = width // TILE

    def target(j):
        low = jnp.where(j < n_sub - 1 - z, n_sub - 1 - j, j - (n_sub - 1 - z))
        high = jnp.where(j < z, j, n_sub - 1 - (j - z))
        return jnp.where(z < n_sub // 2, low, high)

    def share(t, k):
        cols = pl.ds(pl.multiple_of(t * width + k * TILE, TILE), TILE)
        return jnp.dot(head[...], w_merge[:, cols], preferred_element_type=F32)

    def hop(t, k):
        up = t > z
        to = jnp.where(up, z + 1, z - 1)
        place = jnp.where(up | (t != z - 1), t, n_sub)
        return remote(sending.at[t, k], landed.at[place, k], hop_send.at[t, k],
                      hop_recv.at[place, k], (s, to))

    for j in range(n_sub - 1):
        t = target(j)
        edge = jnp.where(t > z, z == 0, z == n_sub - 1)

        @pl.loop(0, tiles)
        def _(k):
            total = share(t, k)

            @pl.when(edge)
            def _():
                sending[t, k] = total.astype(BF16)

            @pl.when(~edge)
            def _():
                whole(landed.at[t, k], hop_recv.at[t, k]).wait()
                sending[t, k] = (total + landed[t, k].astype(F32)).astype(BF16)

            hop(t, k).start()

    for k in range(tiles):
        acc[:, k * TILE:(k + 1) * TILE] = share(z, k)
    for place, has in ((z, z > 0), (n_sub, z < n_sub - 1)):
        @pl.when(has)
        def _():
            for k in range(tiles):
                whole(landed.at[place, k], hop_recv.at[place, k]).wait()
                acc[:, k * TILE:(k + 1) * TILE] += landed[place, k].astype(F32)

    out[...] = acc[...].astype(out.dtype)

    whole(route, info_send.at[0]).wait()
    for c in range(CHUNKS):
        whole(mine.at[c], raw_send.at[c]).wait()
        whole(packed.at[0, c, pl.ds(0, peers - 1)], slot_send.at[0, c]).wait()
        for g in range(n_sub):
            @pl.when(seat_here(g))
            def _():
                whole(answers.at[g, c, pl.ds(0, n_seq - 1)], ans_send.at[g, c]).wait()

            @pl.when(~seat_here(g))
            def _():
                whole(answers.at[g, c], ans_send.at[g, c]).wait()

        @pl.when(inner)
        def _():
            for j in range(half):
                whole(packed.at[1 + j, c, pl.ds(0, peers - 1)], slot_send.at[1 + j, c]).wait()
                whole(part_out.at[j, c], part_send.at[j, c]).wait()

    for t in range(n_sub):
        @pl.when(z != t)
        def _():
            for k in range(tiles):
                whole(sending.at[t, k], hop_send.at[t, k]).wait()


def layer(n_seq, n_sub, slots, route, capacity, tokens, w_split, w_in, w_out, w_merge):
    half = n_sub // 2
    rows, width = tokens.shape[0], w_out.shape[1]
    peers, wide, tiles = half * n_seq, width // CHUNKS, width // TILE
    vmem = pl.BlockSpec(memory_space=pltpu.VMEM)
    hbm = pl.BlockSpec(memory_space=pltpu.HBM)

    def buf(*shape, dtype=BF16):
        return pltpu.VMEM(shape, dtype)

    dma = pltpu.SemaphoreType.DMA
    message = (2 * slots, wide // 2)
    return pl.pallas_call(
        functools.partial(layer_kernel, n_seq, n_sub, slots),
        out_shape=jax.ShapeDtypeStruct((rows, width), BF16),
        in_specs=[vmem] * 2 + [hbm] * 5,
        out_specs=vmem,
        scratch_shapes=[
            buf(*tokens.shape),
            buf(CHUNKS, w_split.shape[0], wide),
            buf(*w_in.shape),
            buf(*w_out.shape),
            buf(*w_merge.shape),
            buf(half, *route.shape, dtype=jnp.int32),
            buf(CHUNKS, rows, wide),
            buf(half, CHUNKS, rows, wide),
            buf(1 + half, peers * slots, rows),
            buf(1 + half, rows, peers * slots),
            buf(1 + half, CHUNKS, peers, *message),
            buf(n_sub, CHUNKS, n_seq, *message),
            buf(n_seq * slots, width),
            buf(n_seq * slots, w_out.shape[0]),
            buf(n_sub, CHUNKS, n_seq, *message),
            buf(1 + half, CHUNKS, peers, *message),
            buf(half, CHUNKS, rows, wide),
            buf(CHUNKS, rows, wide),
            buf(rows, width, dtype=F32),
            buf(rows, width),
            buf(n_sub, tiles, rows, TILE),
            buf(n_sub + 1, tiles, rows, TILE),
            dma((CHUNKS + 4,)),
            dma((1,)),
            dma((half,)),
            dma((CHUNKS,)),
            dma((half, CHUNKS)),
            dma((1 + half, CHUNKS)),
            dma((n_sub, CHUNKS)),
            dma((n_sub, CHUNKS)),
            dma((1 + half, CHUNKS)),
            dma((half, CHUNKS)),
            dma((CHUNKS,)),
            dma((n_sub, tiles)),
            dma((n_sub + 1, tiles)),
        ],
        compiler_params=pltpu.CompilerParams(
            collective_id=1, has_side_effects=True, vmem_limit_bytes=VMEM_BYTES),
        name="layer",
    )(route, capacity, tokens, w_split, w_in, w_out, w_merge)


def body(n_seq, n_sub, tokens, w_split, w_merge, expert_in, expert_out, expert_ids, combine_q,
         capacity):
    experts = capacity.shape[0]
    slot_count = -(-(3 * tokens.shape[0] // experts) // 8) * 8
    route = jnp.concatenate([expert_ids[0].T, combine_q[0].T], axis=0)
    return layer(n_seq, n_sub, slot_count, route, capacity[None, :], tokens, w_split,
                 expert_in[0], expert_out[0], w_merge)


def solution(mesh):
    in_specs = (
        P("seq", None),
        P(None, "sub"),
        P("sub", None),
        P(("seq", "sub"), None, None),
        P(("seq", "sub"), None, None),
        P("sub", "seq", None),
        P("sub", "seq", None),
        P(),
    )
    out_specs = P("seq", "sub")
    call = functools.partial(body, mesh.shape["seq"], mesh.shape["sub"])
    return jax.shard_map(call, mesh=mesh, in_specs=in_specs, out_specs=out_specs, check_vma=False)
```

time: 127 us -> 115 us (0.906)
  Pallas kernels: 118 us -> 112 us
  matrix products: 5.86 us -> 0 us
  other arithmetic: 0 us -> 1.3 us
    pallas_call x2 -> x1, Pallas kernels: 118 us -> 112 us  [layer(): pl.pallas_call(functools.partial(layer_kernel, n_seq, n_sub, slots), out_...]
    dot_general x1 -> x0, matrix products: 5.86 us -> none  [body(): jnp.dot(tokens, w_split, preferred_element_type=jnp.float32)]
    concatenate x0 -> x1, other arithmetic: none -> 1.3 us  [body(): route = jnp.concatenate([expert_ids[0].T, combine_q[0].T], axis=0)]
where the time goes in v1:
time: 115 us
  Pallas kernels  112 us (97%)
  local copies, waits for them, and re-layouts  1.87 us (2%)
  other arithmetic  1.3 us (1%)
    pallas_call x1, Pallas kernels, layer(): pl.pallas_call(functools.partial(layer_kernel, n_seq, n_sub, slots), out_...  112 us

profile of v1, /device:TPU:0, one launch (start us, length us, event | category | flops | bytes accessed | tf_op | source)
XLA Modules:
  0.0 114.8 jit_solution(11279727759343737049)
XLA Ops:
  0.0 1.3 %pad_add_fusion.route = s32[4,256]{1,0:T(4,128)} fusion(s32[2,256]{1,0:T(2,128)} %bitcast.11, s32[2,256]{1,0:T(2,128)} %bitcast.12), kind=kLoop, calls=%fused_computation | loop fusion | flops 1024 | bytes 8192 | tf_op jit(solution)/shard_map/concatenate | solution.py:411
  1.3 111.6 %layer.1 = bf16[256,1024]{1,0:T(8,128)(2,1)} custom-call(s32[4,256]{1,0:T(4,128)} %pad_add_fusion.route, s32[1,32]{1,0:T(1,128)} %bitcast.13, bf16[256,4096]{1,0:T(8,128)(2,1)} %tokens_hbm.1, bf16[4096,1024]{1,0:T(8,128)(2,1)} %w_split_hbm.1, bf16[1024,2048]{1,0:T(8,128)(2,1)} %bitcast.9, bf16[1024,1024]{1,0:T(8,128)(2,1)} %bitcast.10, ...), custom_call_target="tpu_custom_call" | custom-call | tf_op jit(solution)/shard_map/layer/pallas_call | solution.py:359
  112.9 1.9 %copy.10 = bf16[256,1024]{1,0:T(8,128)(2,1)} copy(bf16[256,1024]{1,0:T(8,128)(2,1)} %layer.1) | data formatting | bytes 1048576

commit v2 on v1

v2 whole, which is shorter than its diff:
```python
import functools

import jax
import jax.numpy as jnp
from jax import lax
from jax.experimental import pallas as pl
from jax.experimental.pallas import tpu as pltpu
from jax.sharding import PartitionSpec as P

MESH = pl.DeviceIdType.MESH
scope = jax.named_scope
TILE = 256
CHUNKS = 2
PARTS = 2 * CHUNKS
EARLY = 1
VMEM_BYTES = 60 * 1024 * 1024
F32 = jnp.float32
BF16 = jnp.bfloat16


def layer_kernel(n_seq, n_sub, slots, route, capacity, tokens_hbm, w_split_hbm, w_in_hbm,
                 w_out_hbm, w_merge_hbm, out,
                 tokens, w_split, w_in, w_out, w_merge, info, mine, raw, pick, mix, packed,
                 received, x, hidden, answers, returned, part_out, part_in, acc, head,
                 sending, landed,
                 load_sem, info_send, info_recv, raw_send, raw_recv, slot_send, slot_recv,
                 ans_send, ans_recv, back_send, back_recv, part_send, part_recv,
                 hop_send, hop_recv):
    s, z = lax.axis_index("seq"), lax.axis_index("sub")
    half = n_sub // 2
    last = half - 1
    side = z // half
    q = jnp.where(side == 0, z, n_sub - 1 - z)
    inner = q == last
    n = n_seq * n_sub
    peers = half * n_seq
    rows, width = acc.shape
    part = width // PARTS
    ffe = w_out.shape[0]
    group = n_seq * slots
    outers = range(last)

    def plane(where, depth):
        return jnp.where(where == 0, depth, n_sub - 1 - depth)

    def near(r, depth):
        return (lax.rem(s + r, n_seq), plane(side, depth))

    def across():
        return (s, plane(1 - side, last))

    fetch_tokens = pltpu.make_async_copy(tokens_hbm, tokens, load_sem.at[PARTS])
    fetch_in = pltpu.make_async_copy(w_in_hbm, w_in, load_sem.at[PARTS + 1])
    fetch_out = pltpu.make_async_copy(w_out_hbm, w_out, load_sem.at[PARTS + 2])
    fetch_merge = pltpu.make_async_copy(w_merge_hbm, w_merge, load_sem.at[PARTS + 3])

    def fetch_split(i):
        return pltpu.make_async_copy(
            w_split_hbm.at[:, pl.ds(i * part, part)], w_split.at[i], load_sem.at[i])

    fetch_tokens.start()
    fetch_split(0).start()

    barrier = pltpu.get_barrier_semaphore()
    for p in range(half):
        @pl.loop(0, n_seq)
        def _(r):
            @pl.when((r != 0) | (q != p))
            def _():
                pl.semaphore_signal(barrier, inc=1, device_id=near(r, p), device_id_type=MESH)

        @pl.when(inner | (p == last))
        def _():
            pl.semaphore_signal(barrier, inc=1, device_id=(s, plane(1 - side, p)),
                                device_id_type=MESH)

    def remote(src, dst, send, recv, to):
        return pltpu.make_async_remote_copy(src_ref=src, dst_ref=dst, send_sem=send,
                                            recv_sem=recv, device_id=to, device_id_type=MESH)

    def whole(ref, sem):
        return pltpu.make_async_copy(ref, ref, sem)

    def info_near():
        return remote(route, info.at[q], info_send.at[0], info_recv.at[q], (s, plane(side, last)))

    def info_across():
        return remote(route, info.at[half + q], info_send.at[1], info_recv.at[half + q], across())

    def raw_across(i):
        return remote(mine.at[i], raw.at[q, i], raw_send.at[i], raw_recv.at[q, i], across())

    def part_across(g, i):
        return remote(part_out.at[half + g, i], part_in.at[g, i], part_send.at[half + g, i],
                      part_recv.at[g, i], across())

    def part_outward(g, i):
        return remote(part_out.at[g, i], part_in.at[g, i], part_send.at[g, i],
                      part_recv.at[g, i], (s, plane(side, g)))

    def ship(g, c, p):
        with scope("ship"):
            @pl.loop(0, n_seq)
            def _(r):
                @pl.when((r != 0) | (q != p))
                def _():
                    remote(packed.at[g, c, p, r], received.at[g, c, r], slot_send.at[g, c, p],
                           slot_recv.at[g, c], near(r, p)).start()

            @pl.when(q == p)
            def _():
                received[g, c, 0:1] = packed[g, c, p, 0:1]

    def unfold(y):
        y = y.astype(F32)
        return (y[:, :slots].reshape(group, part).astype(BF16),
                y[:, slots:].reshape(group, part).astype(BF16))

    def pack(g, p, block, c):
        with scope("pack"):
            y = [jnp.dot(pick[g, p], block(2 * c + k), preferred_element_type=F32)
                 .reshape(n_seq, slots, part) for k in range(2)]
            packed[g, c, p] = jnp.concatenate(y, axis=1).astype(BF16)

    square = lax.broadcasted_iota(jnp.int32, (n, n), 0)
    cross = lax.broadcasted_iota(jnp.int32, (n, n), 1)
    limit = jnp.sum(jnp.where(square == cross, capacity[...].astype(F32), 0.0),
                    axis=1, keepdims=True)
    expert = lax.broadcasted_iota(jnp.int32, (n, 1), 0).astype(F32)
    expert_seq = jnp.floor((expert + 0.5) / n_sub)
    expert_sub = (expert - expert_seq * n_sub).astype(jnp.int32)
    away = expert_seq.astype(jnp.int32) - s
    away = jnp.where(away < 0, away + n_seq, away)
    depth = jnp.where(side == 0, expert_sub, n_sub - 1 - expert_sub)
    seats = jnp.where(depth < half, (depth * n_seq + away) * slots, -1).astype(F32)

    def tables(ids, g, wanted):
        places = lax.broadcasted_iota(jnp.int32, (n, rows), 0)
        named = [(places == ids[k:k + 1, :]).astype(F32) for k in range(2)]
        before = (lax.broadcasted_iota(jnp.int32, (rows, rows), 0)
                  < lax.broadcasted_iota(jnp.int32, (rows, rows), 1))
        earlier = jnp.dot((named[0] + named[1]).astype(BF16), before.astype(F32).astype(BF16),
                          preferred_element_type=F32)
        slot, weight = [], []
        for k in range(2):
            rank = jnp.sum(named[k] * earlier, axis=0, keepdims=True)
            most = jnp.sum(named[k] * limit, axis=0, keepdims=True)
            seat = jnp.sum(named[k] * seats, axis=0, keepdims=True)
            kept = (rank < most) & (seat >= 0.0)
            slot.append(jnp.where(kept, seat + rank, -1.0).astype(jnp.int32))
            weight.append(ids[2 + k:3 + k, :].astype(F32) / 65536.0)
        for p in range(half):
            if wanted(p):
                at = lax.broadcasted_iota(jnp.int32, (group, rows), 0) + p * group
                first, second = at == slot[0], at == slot[1]
                pick[g, p] = (jnp.where(first, 1.0, 0.0) + jnp.where(second, 1.0, 0.0)).astype(BF16)
                full = jnp.where(first, weight[0], 0.0) + jnp.where(second, weight[1], 0.0)
                mix[g, p] = full.T.astype(BF16)

    with scope("tables"):
        tables(route[...], q, lambda p: True)

    with scope("w_tokens"):
        fetch_tokens.wait()
    for i in range(1, PARTS):
        fetch_split(i).start()
    fetch_in.start()
    fetch_out.start()

    def pack_own(c):
        for p in range(half):
            pack(q, p, lambda i: mine[i], c)

            @pl.when(inner | (q == p))
            def _():
                ship(q, c, p)

    for i in range(PARTS):
        with scope("w_split"):
            fetch_split(i).wait()
        with scope("split"):
            mine[i] = jnp.dot(tokens[...], w_split[i], preferred_element_type=F32).astype(BF16)
        if i == 0:
            with scope("w_barrier"):
                pl.semaphore_wait(barrier, peers - 1 + jnp.where(inner, half, 1))
            info_across().start()

            @pl.when(~inner)
            def _():
                info_near().start()

        @pl.when(~inner | (half == 1) | (i < EARLY))
        def _():
            raw_across(i).start()

        if i % 2 == 1:
            @pl.when(inner)
            def _():
                pack_own(i // 2)

    fetch_merge.start()

    def proxy(g, c):
        for i in (2 * c, 2 * c + 1):
            with scope(f"w_raw{g}"):
                whole(raw.at[g - half, i], raw_recv.at[g - half, i]).wait()
        for p in range(half):
            pack(g, p, lambda i: raw[g - half, i], c)
            ship(g, c, p)

    def ffn(k, g):
        for c in range(CHUNKS):
            with scope(f"w_slots{k}"):
                direct = q != jnp.minimum(g, last)

                @pl.when(direct)
                def _():
                    whole(received.at[g, c], slot_recv.at[g, c]).wait()

                @pl.when(jnp.logical_not(direct))
                def _():
                    whole(received.at[g, c, pl.ds(0, n_seq - 1)], slot_recv.at[g, c]).wait()
            with scope("unfold"):
                left, right = unfold(received[g, c])
                x[:, 2 * c * part:(2 * c + 1) * part] = left
                x[:, (2 * c + 1) * part:(2 * c + 2) * part] = right

        with scope("gate_up"):
            @pl.loop(0, ffe // TILE)
            def _(t):
                gate_at = pl.ds(pl.multiple_of(t * TILE, TILE), TILE)
                up_at = pl.ds(pl.multiple_of(ffe + t * TILE, TILE), TILE)
                gate = jnp.dot(x[...], w_in[:, gate_at], preferred_element_type=F32)
                up = jnp.dot(x[...], w_in[:, up_at], preferred_element_type=F32)
                hidden[:, gate_at] = (gate / (1.0 + jnp.exp(-gate)) * up).astype(BF16)

        for c in range(CHUNKS):
            with scope("down"):
                y = [jnp.dot(hidden[...], w_out[:, i * part:(i + 1) * part],
                             preferred_element_type=F32).reshape(n_seq, slots, part)
                     for i in (2 * c, 2 * c + 1)]
                answers[g, c] = jnp.concatenate(y, axis=1).astype(BF16)

    def reply(g):
        for c in range(CHUNKS):
            with scope("reply"):
                @pl.loop(1, n_seq)
                def _(r):
                    remote(answers.at[g, c, r], returned.at[g, c, q * n_seq + r],
                           ans_send.at[g, c], ans_recv.at[g, c], near(n_seq - r, q)).start()

                returned[g, c, pl.ds(q * n_seq, 1)] = answers[g, c, 0:1]

    def mine_at(g, c, p):
        return returned.at[g, c, pl.ds(p * n_seq, n_seq)]

    def gathered(g, c):
        with scope("w_gather"):
            whole(returned.at[g, c, pl.ds(0, n_seq - 1)], ans_recv.at[g, c]).wait()

    def inward(g, c):
        return remote(mine_at(g, c, q), mine_at(g, c, q), back_send.at[g, c],
                      back_recv.at[g, c, q], (s, plane(side, last)))

    def pass_inward(g):
        for c in range(CHUNKS):
            gathered(g, c)
            inward(g, c).start()

    def combine(g, c, planes, tag):
        gathered(g, c)
        with scope(f"w_reply{tag}"):
            for p in planes:
                if p != last:
                    whole(mine_at(g, c, p), back_recv.at[g, c, p]).wait()
        with scope("combine"):
            total = [None, None]
            for p in planes:
                halves = unfold(returned[g, c, pl.ds(p * n_seq, n_seq)])
                for k in range(2):
                    y = jnp.dot(mix[g, p], halves[k], preferred_element_type=F32)
                    total[k] = y if total[k] is None else total[k] + y
            return total

    every = list(range(half))

    def bring_across(g):
        for c in range(CHUNKS):
            sums = combine(half + g, c, every, half + g)
            for k in range(2):
                part_out[half + g, 2 * c + k] = sums[k].astype(BF16)
                part_across(g, 2 * c + k).start()

    def bring_outward(g):
        for c in range(CHUNKS):
            sums = combine(g, c, [p for p in every if p != g], g)
            for k in range(2):
                i = 2 * c + k
                with scope("w_part"):
                    whole(part_in.at[g, i], part_recv.at[g, i]).wait()
                part_out[g, i] = (sums[k] + part_in[g, i].astype(F32)).astype(BF16)
                part_outward(g, i).start()

    def learn(g):
        with scope("w_info"):
            whole(info.at[g], info_recv.at[g]).wait()
        with scope("tables"):
            tables(info[g], g, lambda p: p != g)

    with scope("w_load"):
        fetch_in.wait()
        fetch_out.wait()

    @pl.when(inner)
    def _():
        learn(half)
        proxy(half, 0)
        ffn(0, last)
        for c in range(1, CHUNKS):
            proxy(half, c)
        if half > 1:
            for i in range(EARLY, PARTS):
                raw_across(i).start()
        for g in [*range(half + 1, n_sub), *outers]:
            learn(g)
        for g in range(half + 1, n_sub):
            proxy(g, 0)
            ffn(g - 1, g - 1)
            for c in range(1, CHUNKS):
                proxy(g, c)
            reply(g - 1)
        for g in outers:
            ffn(1 + g, g)
        ffn(n_sub - 1, n_sub - 1)
        for g in outers:
            reply(g)
        reply(n_sub - 1)
        reply(last)
        for g in outers:
            bring_across(g)
        for g in outers:
            bring_outward(g)
        bring_across(last)
        for c in range(CHUNKS):
            sums = combine(last, c, every, "own")
            for k in range(2):
                i = 2 * c + k
                acc[:, i * part:(i + 1) * part] = sums[k]

    @pl.when(~inner)
    def _():
        for c in range(CHUNKS):
            pack_own(c)
        with scope("w_sent"):
            for i in range(PARTS):
                whole(mine.at[i], raw_send.at[i]).wait()
        for c in range(CHUNKS):
            for p in range(half):
                @pl.when(q != p)
                def _():
                    ship(q, c, p)

        ffn(1, last)
        reply(last)
        ffn(0, q)
        pass_inward(last)
        for g in range(half, n_sub):
            ffn(g, g)
            reply(g)
            pass_inward(g)
            if g == half:
                reply(q)

        for g in outers:
            @pl.when(q != g)
            def _():
                ffn(n_sub, g)
                reply(g)
                pass_inward(g)

    for g in outers:
        @pl.when(q == g)
        def _():
            for c in range(CHUNKS):
                gathered(g, c)
                halves = unfold(returned[g, c, pl.ds(g * n_seq, n_seq)])
                for k in range(2):
                    i = 2 * c + k
                    acc[:, i * part:(i + 1) * part] = jnp.dot(
                        mix[g, g], halves[k], preferred_element_type=F32)

    for i in range(PARTS):
        at = slice(i * part, (i + 1) * part)
        with scope("w_part"):
            whole(part_in.at[q, i], part_recv.at[q, i]).wait()
        head[:, at] = (acc[:, at] + part_in[q, i].astype(F32)).astype(BF16)

    with scope("w_merge"):
        fetch_merge.wait()
    tiles = width // TILE

    def target(j):
        low = jnp.where(j < n_sub - 1 - z, n_sub - 1 - j, j - (n_sub - 1 - z))
        high = jnp.where(j < z, j, n_sub - 1 - (j - z))
        return jnp.where(z < n_sub // 2, low, high)

    def share(t, k):
        cols = pl.ds(pl.multiple_of(t * width + k * TILE, TILE), TILE)
        return jnp.dot(head[...], w_merge[:, cols], preferred_element_type=F32)

    def hop(t, k):
        up = t > z
        to = jnp.where(up, z + 1, z - 1)
        place = jnp.where(up | (t != z - 1), t, n_sub)
        return remote(sending.at[t, k], landed.at[place, k], hop_send.at[t, k],
                      hop_recv.at[place, k], (s, to))

    for j in range(n_sub - 1):
        t = target(j)
        edge = jnp.where(t > z, z == 0, z == n_sub - 1)

        with scope(f"merge{j}"):
            @pl.loop(0, tiles)
            def _(k):
                total = share(t, k)

                @pl.when(edge)
                def _():
                    sending[t, k] = total.astype(BF16)

                @pl.when(~edge)
                def _():
                    whole(landed.at[t, k], hop_recv.at[t, k]).wait()
                    sending[t, k] = (total + landed[t, k].astype(F32)).astype(BF16)

                hop(t, k).start()

    with scope("merge_own"):
        for k in range(tiles):
            acc[:, k * TILE:(k + 1) * TILE] = share(z, k)
    for place, has in ((z, z > 0), (n_sub, z < n_sub - 1)):
        with scope("w_landed"):
            @pl.when(has)
            def _():
                for k in range(tiles):
                    whole(landed.at[place, k], hop_recv.at[place, k]).wait()
                    acc[:, k * TILE:(k + 1) * TILE] += landed[place, k].astype(F32)

    with scope("finish"):
        out[...] = acc[...].astype(out.dtype)

    whole(route, info_send.at[1]).wait()

    @pl.when(~inner)
    def _():
        whole(route, info_send.at[0]).wait()

    @pl.when(inner)
    def _():
        for i in range(PARTS):
            whole(mine.at[i], raw_send.at[i]).wait()

    for g in range(n_sub):
        sender = (q == g) | (inner & (g >= half))
        for c in range(CHUNKS):
            whole(answers.at[g, c, pl.ds(0, n_seq - 1)], ans_send.at[g, c]).wait()

            @pl.when(~inner & (q != g))
            def _():
                whole(mine_at(g, c, q), back_send.at[g, c]).wait()

            for p in range(half):
                @pl.when(sender & (q == p))
                def _():
                    whole(received.at[g, c, pl.ds(0, n_seq - 1)], slot_send.at[g, c, p]).wait()

                @pl.when(sender & (q != p))
                def _():
                    whole(received.at[g, c], slot_send.at[g, c, p]).wait()

    @pl.when(inner)
    def _():
        for g in range(n_sub):
            for i in range(PARTS):
                if g != last:
                    whole(part_out.at[g, i], part_send.at[g, i]).wait()

    for t in range(n_sub):
        @pl.when(z != t)
        def _():
            for k in range(tiles):
                whole(sending.at[t, k], hop_send.at[t, k]).wait()


def layer(n_seq, n_sub, slots, route, capacity, tokens, w_split, w_in, w_out, w_merge):
    half = n_sub // 2
    rows, width = tokens.shape[0], w_out.shape[1]
    peers, part, tiles = half * n_seq, width // PARTS, width // TILE
    vmem = pl.BlockSpec(memory_space=pltpu.VMEM)
    hbm = pl.BlockSpec(memory_space=pltpu.HBM)

    def buf(*shape, dtype=BF16):
        return pltpu.VMEM(shape, dtype)

    dma = pltpu.SemaphoreType.DMA
    message = (2 * slots, part)
    group = n_seq * slots
    return pl.pallas_call(
        functools.partial(layer_kernel, n_seq, n_sub, slots),
        out_shape=jax.ShapeDtypeStruct((rows, width), BF16),
        in_specs=[vmem] * 2 + [hbm] * 5,
        out_specs=vmem,
        scratch_shapes=[
            buf(*tokens.shape),
            buf(PARTS, w_split.shape[0], part),
            buf(*w_in.shape),
            buf(*w_out.shape),
            buf(*w_merge.shape),
            buf(n_sub, *route.shape, dtype=jnp.int32),
            buf(PARTS, rows, part),
            buf(half, PARTS, rows, part),
            buf(n_sub, half, group, rows),
            buf(n_sub, half, rows, group),
            buf(n_sub, CHUNKS, half, n_seq, *message),
            buf(n_sub, CHUNKS, n_seq, *message),
            buf(group, width),
            buf(group, w_out.shape[0]),
            buf(n_sub, CHUNKS, n_seq, *message),
            buf(n_sub, CHUNKS, peers, *message),
            buf(n_sub, PARTS, rows, part),
            buf(half, PARTS, rows, part),
            buf(rows, width, dtype=F32),
            buf(rows, width),
            buf(n_sub, tiles, rows, TILE),
            buf(n_sub + 1, tiles, rows, TILE),
            dma((PARTS + 4,)),
            dma((2,)),
            dma((n_sub,)),
            dma((PARTS,)),
            dma((half, PARTS)),
            dma((n_sub, CHUNKS, half)),
            dma((n_sub, CHUNKS)),
            dma((n_sub, CHUNKS)),
            dma((n_sub, CHUNKS)),
            dma((n_sub, CHUNKS)),
            dma((n_sub, CHUNKS, half)),
            dma((n_sub, PARTS)),
            dma((half, PARTS)),
            dma((n_sub, tiles)),
            dma((n_sub + 1, tiles)),
        ],
        compiler_params=pltpu.CompilerParams(
            collective_id=1, has_side_effects=True, vmem_limit_bytes=VMEM_BYTES),
        name="layer",
    )(route, capacity, tokens, w_split, w_in, w_out, w_merge)


def body(n_seq, n_sub, tokens, w_split, w_merge, expert_in, expert_out, expert_ids, combine_q,
         capacity):
    experts = capacity.shape[0]
    slot_count = -(-(3 * tokens.shape[0] // experts) // 8) * 8
    route = jnp.concatenate([expert_ids[0].T, combine_q[0].T], axis=0)
    return layer(n_seq, n_sub, slot_count, route, capacity[None, :], tokens, w_split,
                 expert_in[0], expert_out[0], w_merge)


def solution(mesh):
    in_specs = (
        P("seq", None),
        P(None, "sub"),
        P("sub", None),
        P(("seq", "sub"), None, None),
        P(("seq", "sub"), None, None),
        P("sub", "seq", None),
        P("sub", "seq", None),
        P(),
    )
    out_specs = P("seq", "sub")
    call = functools.partial(body, mesh.shape["seq"], mesh.shape["sub"])
    return jax.shard_map(call, mesh=mesh, in_specs=in_specs, out_specs=out_specs, check_vma=False)
```

time: 115 us -> 103 us (0.90)
  Pallas kernels: 112 us -> 99.2 us
    pallas_call x1, Pallas kernels: 112 us -> 99.2 us  [layer(): pl.pallas_call(functools.partial(layer_kernel, n_seq, n_sub, slots), out_...]
where the time goes in v2:
time: 103 us; the launch traced here: 102 us
  Pallas kernels  99.2 us (96%)
  local copies, waits for them, and re-layouts  1.87 us (2%)
  other arithmetic  1.3 us (1%)
    pallas_call x1, Pallas kernels, layer(): pl.pallas_call(functools.partial(layer_kernel, n_seq, n_sub, slots), out_...  99.2 us

profile of v2, /device:TPU:0, one launch (start us, length us, event | category | flops | bytes accessed | tf_op | source)
XLA Modules:
  0.0 102.4 jit_solution(7012534561881719824)
XLA Ops:
  0.0 1.3 %pad_add_fusion.route = s32[4,256]{1,0:T(4,128)} fusion(s32[2,256]{1,0:T(2,128)} %bitcast.11, s32[2,256]{1,0:T(2,128)} %bitcast.12), kind=kLoop, calls=%fused_computation | loop fusion | flops 1024 | bytes 8192 | tf_op jit(solution)/shard_map/concatenate | solution.py:562
  1.3 99.2 %layer.1 = bf16[256,1024]{1,0:T(8,128)(2,1)} custom-call(s32[4,256]{1,0:T(4,128)} %pad_add_fusion.route, s32[1,32]{1,0:T(1,128)} %bitcast.13, bf16[256,4096]{1,0:T(8,128)(2,1)} %tokens_hbm.1, bf16[4096,1024]{1,0:T(8,128)(2,1)} %w_split_hbm.1, bf16[1024,2048]{1,0:T(8,128)(2,1)} %bitcast.9, bf16[1024,1024]{1,0:T(8,128)(2,1)} %bitcast.10, ...), custom_call_target="tpu_custom_call" | custom-call | tf_op jit(solution)/shard_map/layer/pallas_call | solution.py:508
  100.5 1.9 %copy.10 = bf16[256,1024]{1,0:T(8,128)(2,1)} copy(bf16[256,1024]{1,0:T(8,128)(2,1)} %layer.1) | data formatting | bytes 1048576

commit v3 on v2

--- a/solution.py
+++ b/solution.py
@@ -18,9 +18,9 @@
 BF16 = jnp.bfloat16
 
 
-def layer_kernel(n_seq, n_sub, slots, route, capacity, tokens_hbm, w_split_hbm, w_in_hbm,
+def layer_kernel(n_seq, n_sub, slots, ids_hbm, quanta_hbm, capacity, tokens_hbm, w_split_hbm, w_in_hbm,
                  w_out_hbm, w_merge_hbm, out,
-                 tokens, w_split, w_in, w_out, w_merge, info, mine, raw, pick, mix, packed,
+                 tokens, w_split, w_in, w_out, w_merge, route, info, mine, raw, pick, mix, packed,
                  received, x, hidden, answers, returned, part_out, part_in, acc, head,
                  sending, landed,
                  load_sem, info_send, info_recv, raw_send, raw_recv, slot_send, slot_recv,
@@ -58,6 +58,10 @@
         return pltpu.make_async_copy(
             w_split_hbm.at[:, pl.ds(i * part, part)], w_split.at[i], load_sem.at[i])
 
+    fetch_ids = pltpu.make_async_copy(ids_hbm, route.at[0], load_sem.at[PARTS + 4])
+    fetch_quanta = pltpu.make_async_copy(quanta_hbm, route.at[1], load_sem.at[PARTS + 5])
+    fetch_ids.start()
+    fetch_quanta.start()
     fetch_tokens.start()
     fetch_split(0).start()
 
@@ -136,7 +140,7 @@
 
     def tables(ids, g, wanted):
         places = lax.broadcasted_iota(jnp.int32, (n, rows), 0)
-        named = [(places == ids[k:k + 1, :]).astype(F32) for k in range(2)]
+        named = [(places == ids[0, k:k + 1, :]).astype(F32) for k in range(2)]
         before = (lax.broadcasted_iota(jnp.int32, (rows, rows), 0)
                   < lax.broadcasted_iota(jnp.int32, (rows, rows), 1))
         earlier = jnp.dot((named[0] + named[1]).astype(BF16), before.astype(F32).astype(BF16),
@@ -148,7 +152,7 @@
             seat = jnp.sum(named[k] * seats, axis=0, keepdims=True)
             kept = (rank < most) & (seat >= 0.0)
             slot.append(jnp.where(kept, seat + rank, -1.0).astype(jnp.int32))
-            weight.append(ids[2 + k:3 + k, :].astype(F32) / 65536.0)
+            weight.append(ids[1, k:k + 1, :].astype(F32) / 65536.0)
         for p in range(half):
             if wanted(p):
                 at = lax.broadcasted_iota(jnp.int32, (group, rows), 0) + p * group
@@ -157,8 +161,11 @@
                 full = jnp.where(first, weight[0], 0.0) + jnp.where(second, weight[1], 0.0)
                 mix[g, p] = full.T.astype(BF16)
 
+    with scope("w_route"):
+        fetch_ids.wait()
+        fetch_quanta.wait()
     with scope("tables"):
-        tables(route[...], q, lambda p: True)
+        tables(route, q, lambda p: True)
 
     with scope("w_tokens"):
         fetch_tokens.wait()
@@ -208,7 +215,7 @@
             pack(g, p, lambda i: raw[g - half, i], c)
             ship(g, c, p)
 
-    def ffn(k, g):
+    def ffn(k, g, meanwhile=None):
         for c in range(CHUNKS):
             with scope(f"w_slots{k}"):
                 direct = q != jnp.minimum(g, last)
@@ -225,6 +232,8 @@
                 x[:, 2 * c * part:(2 * c + 1) * part] = left
                 x[:, (2 * c + 1) * part:(2 * c + 2) * part] = right
 
+        if meanwhile is not None:
+            meanwhile()
         with scope("gate_up"):
             @pl.loop(0, ffe // TILE)
             def _(t):
@@ -241,15 +250,25 @@
                      for i in (2 * c, 2 * c + 1)]
                 answers[g, c] = jnp.concatenate(y, axis=1).astype(BF16)
 
+    def paced(g, c):
+        return isinstance(g, int) and g >= half and c < CHUNKS - 1
+
+    def reply_chunk(g, c):
+        with scope("reply"):
+            @pl.loop(1, n_seq)
+            def _(r):
+                remote(answers.at[g, c, r], returned.at[g, c, q * n_seq + r],
+                       ans_send.at[g, c], ans_recv.at[g, c], near(n_seq - r, q)).start()
+
+            returned[g, c, pl.ds(q * n_seq, 1)] = answers[g, c, 0:1]
+
     def reply(g):
         for c in range(CHUNKS):
-            with scope("reply"):
-                @pl.loop(1, n_seq)
-                def _(r):
-                    remote(answers.at[g, c, r], returned.at[g, c, q * n_seq + r],
-                           ans_send.at[g, c], ans_recv.at[g, c], near(n_seq - r, q)).start()
-
-                returned[g, c, pl.ds(q * n_seq, 1)] = answers[g, c, 0:1]
+            reply_chunk(g, c)
+
+    def left(g, c):
+        with scope("w_left"):
+            whole(answers.at[g, c, pl.ds(0, n_seq - 1)], ans_send.at[g, c]).wait()
 
     def mine_at(g, c, p):
         return returned.at[g, c, pl.ds(p * n_seq, n_seq)]
@@ -262,8 +281,8 @@
         return remote(mine_at(g, c, q), mine_at(g, c, q), back_send.at[g, c],
                       back_recv.at[g, c, q], (s, plane(side, last)))
 
-    def pass_inward(g):
-        for c in range(CHUNKS):
+    def pass_inward(g, chunks=range(CHUNKS)):
+        for c in chunks:
             gathered(g, c)
             inward(g, c).start()
 
@@ -305,7 +324,7 @@
         with scope("w_info"):
             whole(info.at[g], info_recv.at[g]).wait()
         with scope("tables"):
-            tables(info[g], g, lambda p: p != g)
+            tables(info.at[g], g, lambda p: p != g)
 
     with scope("w_load"):
         fetch_in.wait()
@@ -351,6 +370,7 @@
     def _():
         for c in range(CHUNKS):
             pack_own(c)
+        ffn(1, last)
         with scope("w_sent"):
             for i in range(PARTS):
                 whole(mine.at[i], raw_send.at[i]).wait()
@@ -360,16 +380,23 @@
                 def _():
                     ship(q, c, p)
 
-        ffn(1, last)
-        reply(last)
         ffn(0, q)
-        pass_inward(last)
         for g in range(half, n_sub):
-            ffn(g, g)
-            reply(g)
+            spare = [c for c in range(CHUNKS) if min(c, last) == g - half]
+
+            def meanwhile():
+                for c in spare:
+                    reply_chunk(last, c)
+
+            ffn(g, g, meanwhile)
+            for c in range(CHUNKS):
+                reply_chunk(g, c)
+                if c == 0:
+                    pass_inward(last, spare)
+                if paced(g, c):
+                    left(g, c)
             pass_inward(g)
-            if g == half:
-                reply(q)
+        reply(q)
 
         for g in outers:
             @pl.when(q != g)
@@ -400,9 +427,11 @@
     tiles = width // TILE
 
     def target(j):
-        low = jnp.where(j < n_sub - 1 - z, n_sub - 1 - j, j - (n_sub - 1 - z))
-        high = jnp.where(j < z, j, n_sub - 1 - (j - z))
-        return jnp.where(z < n_sub // 2, low, high)
+        y = jnp.where(z < half, z, n_sub - 1 - z)
+        far = n_sub - 2 - y
+        t = jnp.where(j < far, n_sub - 1 - j, j - far)
+        t = jnp.where(j == n_sub - 2, y + 1, jnp.where(j == n_sub - 1, y, t))
+        return jnp.where(z < half, t, n_sub - 1 - t)
 
     def share(t, k):
         cols = pl.ds(pl.multiple_of(t * width + k * TILE, TILE), TILE)
@@ -438,17 +467,6 @@
     with scope("merge_own"):
         for k in range(tiles):
             acc[:, k * TILE:(k + 1) * TILE] = share(z, k)
-    for place, has in ((z, z > 0), (n_sub, z < n_sub - 1)):
-        with scope("w_landed"):
-            @pl.when(has)
-            def _():
-                for k in range(tiles):
-                    whole(landed.at[place, k], hop_recv.at[place, k]).wait()
-                    acc[:, k * TILE:(k + 1) * TILE] += landed[place, k].astype(F32)
-
-    with scope("finish"):
-        out[...] = acc[...].astype(out.dtype)
-
     whole(route, info_send.at[1]).wait()
 
     @pl.when(~inner)
@@ -463,7 +481,9 @@
     for g in range(n_sub):
         sender = (q == g) | (inner & (g >= half))
         for c in range(CHUNKS):
-            whole(answers.at[g, c, pl.ds(0, n_seq - 1)], ans_send.at[g, c]).wait()
+            @pl.when(inner | (not paced(g, c)))
+            def _():
+                whole(answers.at[g, c, pl.ds(0, n_seq - 1)], ans_send.at[g, c]).wait()
 
             @pl.when(~inner & (q != g))
             def _():
@@ -485,6 +505,17 @@
                 if g != last:
                     whole(part_out.at[g, i], part_send.at[g, i]).wait()
 
+    for place, has in ((z, z > 0), (n_sub, z < n_sub - 1)):
+        with scope("w_landed"):
+            @pl.when(has)
+            def _():
+                for k in range(tiles):
+                    whole(landed.at[place, k], hop_recv.at[place, k]).wait()
+                    acc[:, k * TILE:(k + 1) * TILE] += landed[place, k].astype(F32)
+
+    with scope("finish"):
+        out[...] = acc[...].astype(out.dtype)
+
     for t in range(n_sub):
         @pl.when(z != t)
         def _():
@@ -492,7 +523,7 @@
                 whole(sending.at[t, k], hop_send.at[t, k]).wait()
 
 
-def layer(n_seq, n_sub, slots, route, capacity, tokens, w_split, w_in, w_out, w_merge):
+def layer(n_seq, n_sub, slots, ids, quanta, capacity, tokens, w_split, w_in, w_out, w_merge):
     half = n_sub // 2
     rows, width = tokens.shape[0], w_out.shape[1]
     peers, part, tiles = half * n_seq, width // PARTS, width // TILE
@@ -508,7 +539,7 @@
     return pl.pallas_call(
         functools.partial(layer_kernel, n_seq, n_sub, slots),
         out_shape=jax.ShapeDtypeStruct((rows, width), BF16),
-        in_specs=[vmem] * 2 + [hbm] * 5,
+        in_specs=[hbm] * 2 + [vmem] + [hbm] * 5,
         out_specs=vmem,
         scratch_shapes=[
             buf(*tokens.shape),
@@ -516,7 +547,8 @@
             buf(*w_in.shape),
             buf(*w_out.shape),
             buf(*w_merge.shape),
-            buf(n_sub, *route.shape, dtype=jnp.int32),
+            buf(2, *ids.shape, dtype=jnp.int32),
+            buf(n_sub, 2, *ids.shape, dtype=jnp.int32),
             buf(PARTS, rows, part),
             buf(half, PARTS, rows, part),
             buf(n_sub, half, group, rows),
@@ -533,7 +565,7 @@
             buf(rows, width),
             buf(n_sub, tiles, rows, TILE),
             buf(n_sub + 1, tiles, rows, TILE),
-            dma((PARTS + 4,)),
+            dma((PARTS + 6,)),
             dma((2,)),
             dma((n_sub,)),
             dma((PARTS,)),
@@ -552,16 +584,15 @@
         compiler_params=pltpu.CompilerParams(
             collective_id=1, has_side_effects=True, vmem_limit_bytes=VMEM_BYTES),
         name="layer",
-    )(route, capacity, tokens, w_split, w_in, w_out, w_merge)
+    )(ids, quanta, capacity, tokens, w_split, w_in, w_out, w_merge)
 
 
 def body(n_seq, n_sub, tokens, w_split, w_merge, expert_in, expert_out, expert_ids, combine_q,
          capacity):
     experts = capacity.shape[0]
     slot_count = -(-(3 * tokens.shape[0] // experts) // 8) * 8
-    route = jnp.concatenate([expert_ids[0].T, combine_q[0].T], axis=0)
-    return layer(n_seq, n_sub, slot_count, route, capacity[None, :], tokens, w_split,
-                 expert_in[0], expert_out[0], w_merge)
+    return layer(n_seq, n_sub, slot_count, expert_ids[0].T, combine_q[0].T, capacity[None, :],
+                 tokens, w_split, expert_in[0], expert_out[0], w_merge)
 
 
 def solution(mesh):

time: 103 us -> 98.8 us (0.959)
  Pallas kernels: 99.2 us -> 96.1 us
  other arithmetic: 1.3 us -> 0 us
    pallas_call x1, Pallas kernels: 99.2 us -> 96.1 us  [layer(): pl.pallas_call(functools.partial(layer_kernel, n_seq, n_sub, slots), out_...]
    concatenate x1 -> x0, other arithmetic: 1.3 us -> none  [body(): route = jnp.concatenate([expert_ids[0].T, combine_q[0].T], axis=0)]
where the time goes in v3:
time: 98.8 us; the launch traced here: 97.9 us
  Pallas kernels  96.1 us (97%)
  local copies, waits for them, and re-layouts  1.87 us (2%)
    pallas_call x1, Pallas kernels, layer(): pl.pallas_call(functools.partial(layer_kernel, n_seq, n_sub, slots), out_...  96.1 us

profile of v3, /device:TPU:0, one launch (start us, length us, event | category | flops | bytes accessed | tf_op | source)
XLA Modules:
  0.0 97.9 jit_solution(11253255604847492914)
XLA Ops:
  0.0 96.1 %layer.1 = bf16[256,1024]{1,0:T(8,128)(2,1)} custom-call(s32[2,256]{1,0:T(2,128)} %bitcast.11, s32[2,256]{1,0:T(2,128)} %bitcast.12, s32[1,32]{1,0:T(1,128)} %bitcast.13, bf16[256,4096]{1,0:T(8,128)(2,1)} %tokens_hbm.1, bf16[4096,1024]{1,0:T(8,128)(2,1)} %w_split_hbm.1, bf16[1024,2048]{1,0:T(8,128)(2,1)} %bitcast.9, bf16[1024,1024]{1,0:T(8,128)(2,1)} %bitcast.10, ...), custom_call_target="tpu_custom_call" | custom-call | tf_op jit(solution)/shard_map/layer/pallas_call | solution.py:539
  96.1 1.9 %copy.10 = bf16[256,1024]{1,0:T(8,128)(2,1)} copy(bf16[256,1024]{1,0:T(8,128)(2,1)} %layer.1) | data formatting | bytes 1048576

commit v4 on v3

--- a/solution.py
+++ b/solution.py
@@ -12,6 +12,7 @@
 TILE = 256
 CHUNKS = 2
 PARTS = 2 * CHUNKS
+SLABS = 2
 EARLY = 1
 VMEM_BYTES = 60 * 1024 * 1024
 F32 = jnp.float32
@@ -49,7 +50,18 @@
     def across():
         return (s, plane(1 - side, last))
 
-    fetch_tokens = pltpu.make_async_copy(tokens_hbm, tokens, load_sem.at[PARTS])
+    deep = tokens.shape[1] // 2
+
+    def fetch_tokens(k):
+        at = pl.ds(k * deep, deep)
+        return pltpu.make_async_copy(tokens_hbm.at[:, at], tokens.at[:, at],
+                                     load_sem.at[(PARTS, PARTS + 6)[k]])
+
+    def fetch_first(k):
+        at = pl.ds(k * deep, deep)
+        return pltpu.make_async_copy(w_split_hbm.at[at, pl.ds(0, part)], w_split.at[0, at],
+                                     load_sem.at[(0, PARTS + 7)[k]])
+
     fetch_in = pltpu.make_async_copy(w_in_hbm, w_in, load_sem.at[PARTS + 1])
     fetch_out = pltpu.make_async_copy(w_out_hbm, w_out, load_sem.at[PARTS + 2])
     fetch_merge = pltpu.make_async_copy(w_merge_hbm, w_merge, load_sem.at[PARTS + 3])
@@ -62,8 +74,9 @@
     fetch_quanta = pltpu.make_async_copy(quanta_hbm, route.at[1], load_sem.at[PARTS + 5])
     fetch_ids.start()
     fetch_quanta.start()
-    fetch_tokens.start()
-    fetch_split(0).start()
+    for k in range(2):
+        fetch_tokens(k).start()
+        fetch_first(k).start()
 
     barrier = pltpu.get_barrier_semaphore()
     for p in range(half):
@@ -94,13 +107,20 @@
     def raw_across(i):
         return remote(mine.at[i], raw.at[q, i], raw_send.at[i], raw_recv.at[q, i], across())
 
-    def part_across(g, i):
-        return remote(part_out.at[half + g, i], part_in.at[g, i], part_send.at[half + g, i],
-                      part_recv.at[g, i], across())
-
-    def part_outward(g, i):
-        return remote(part_out.at[g, i], part_in.at[g, i], part_send.at[g, i],
-                      part_recv.at[g, i], (s, plane(side, g)))
+    def slab(b):
+        return pl.ds(b * (rows // SLABS), rows // SLABS)
+
+    def part_across(g, i, b):
+        return remote(part_out.at[half + g, i, slab(b)], part_in.at[g, i, slab(b)],
+                      part_send.at[half + g, i, b], part_recv.at[g, i, b], across())
+
+    def part_outward(g, i, b):
+        return remote(part_out.at[g, i, slab(b)], part_in.at[g, i, slab(b)],
+                      part_send.at[g, i, b], part_recv.at[g, i, b], (s, plane(side, g)))
+
+    def part_arrived(g, i, b):
+        with scope("w_part"):
+            whole(part_in.at[g, i, slab(b)], part_recv.at[g, i, b]).wait()
 
     def ship(g, c, p):
         with scope("ship"):
@@ -167,8 +187,6 @@
     with scope("tables"):
         tables(route, q, lambda p: True)
 
-    with scope("w_tokens"):
-        fetch_tokens.wait()
     for i in range(1, PARTS):
         fetch_split(i).start()
     fetch_in.start()
@@ -183,10 +201,22 @@
                 ship(q, c, p)
 
     for i in range(PARTS):
-        with scope("w_split"):
-            fetch_split(i).wait()
-        with scope("split"):
-            mine[i] = jnp.dot(tokens[...], w_split[i], preferred_element_type=F32).astype(BF16)
+        if i == 0:
+            total = None
+            for k in range(2):
+                with scope("w_split"):
+                    fetch_tokens(k).wait()
+                    fetch_first(k).wait()
+                at = slice(k * deep, (k + 1) * deep)
+                y = jnp.dot(tokens[:, at], w_split[0, at], preferred_element_type=F32)
+                total = y if total is None else total + y
+            mine[0] = total.astype(BF16)
+        else:
+            with scope("w_split"):
+                fetch_split(i).wait()
+            with scope("split"):
+                mine[i] = jnp.dot(tokens[...], w_split[i],
+                                  preferred_element_type=F32).astype(BF16)
         if i == 0:
             with scope("w_barrier"):
                 pl.semaphore_wait(barrier, peers - 1 + jnp.where(inner, half, 1))
@@ -308,17 +338,19 @@
             sums = combine(half + g, c, every, half + g)
             for k in range(2):
                 part_out[half + g, 2 * c + k] = sums[k].astype(BF16)
-                part_across(g, 2 * c + k).start()
+                for b in range(SLABS):
+                    part_across(g, 2 * c + k, b).start()
 
     def bring_outward(g):
         for c in range(CHUNKS):
             sums = combine(g, c, [p for p in every if p != g], g)
             for k in range(2):
                 i = 2 * c + k
-                with scope("w_part"):
-                    whole(part_in.at[g, i], part_recv.at[g, i]).wait()
-                part_out[g, i] = (sums[k] + part_in[g, i].astype(F32)).astype(BF16)
-                part_outward(g, i).start()
+                for b in range(SLABS):
+                    part_arrived(g, i, b)
+                    at = slice(b * (rows // SLABS), (b + 1) * (rows // SLABS))
+                    part_out[g, i, at] = (sums[k][at] + part_in[g, i, at].astype(F32)).astype(BF16)
+                    part_outward(g, i, b).start()
 
     def learn(g):
         with scope("w_info"):
@@ -381,21 +413,23 @@
                     ship(q, c, p)
 
         ffn(0, q)
+        rest = range(1, CHUNKS)
+        reply_chunk(last, 0)
+
+        def meanwhile():
+            for c in rest:
+                reply_chunk(last, c)
+
         for g in range(half, n_sub):
-            spare = [c for c in range(CHUNKS) if min(c, last) == g - half]
-
-            def meanwhile():
-                for c in spare:
-                    reply_chunk(last, c)
-
-            ffn(g, g, meanwhile)
+            ffn(g, g, meanwhile if g == n_sub - 1 else None)
             for c in range(CHUNKS):
                 reply_chunk(g, c)
-                if c == 0:
-                    pass_inward(last, spare)
+                if g == half and c == 0:
+                    pass_inward(last, [0])
                 if paced(g, c):
                     left(g, c)
             pass_inward(g)
+        pass_inward(last, rest)
         reply(q)
 
         for g in outers:
@@ -418,8 +452,8 @@
 
     for i in range(PARTS):
         at = slice(i * part, (i + 1) * part)
-        with scope("w_part"):
-            whole(part_in.at[q, i], part_recv.at[q, i]).wait()
+        for b in range(SLABS):
+            part_arrived(q, i, b)
         head[:, at] = (acc[:, at] + part_in[q, i].astype(F32)).astype(BF16)
 
     with scope("w_merge"):
@@ -503,7 +537,8 @@
         for g in range(n_sub):
             for i in range(PARTS):
                 if g != last:
-                    whole(part_out.at[g, i], part_send.at[g, i]).wait()
+                    for b in range(SLABS):
+                        whole(part_out.at[g, i, slab(b)], part_send.at[g, i, b]).wait()
 
     for place, has in ((z, z > 0), (n_sub, z < n_sub - 1)):
         with scope("w_landed"):
@@ -565,7 +600,7 @@
             buf(rows, width),
             buf(n_sub, tiles, rows, TILE),
             buf(n_sub + 1, tiles, rows, TILE),
-            dma((PARTS + 6,)),
+            dma((PARTS + 8,)),
             dma((2,)),
             dma((n_sub,)),
             dma((PARTS,)),
@@ -576,8 +611,8 @@
             dma((n_sub, CHUNKS)),
             dma((n_sub, CHUNKS)),
             dma((n_sub, CHUNKS, half)),
-            dma((n_sub, PARTS)),
-            dma((half, PARTS)),
+            dma((n_sub, PARTS, SLABS)),
+            dma((half, PARTS, SLABS)),
             dma((n_sub, tiles)),
             dma((n_sub + 1, tiles)),
         ],

time: 98.8 us -> 96.1 us (0.973)
  Pallas kernels: 96.1 us -> 94 us
    pallas_call x1, Pallas kernels: 96.1 us -> 94 us  [layer(): pl.pallas_call(functools.partial(layer_kernel, n_seq, n_sub, slots), out_...]
where the time goes in v4:
time: 96.1 us; the launch traced here: 95.9 us
  Pallas kernels  94 us (98%)
  local copies, waits for them, and re-layouts  1.87 us (2%)
    pallas_call x1, Pallas kernels, layer(): pl.pallas_call(functools.partial(layer_kernel, n_seq, n_sub, slots), out_...  94 us

profile of v4, /device:TPU:0, one launch (start us, length us, event | category | flops | bytes accessed | tf_op | source)
XLA Modules:
  0.0 95.9 jit_solution(14489240355990308974)
XLA Ops:
  0.0 94.0 %layer.1 = bf16[256,1024]{1,0:T(8,128)(2,1)} custom-call(s32[2,256]{1,0:T(2,128)} %bitcast.11, s32[2,256]{1,0:T(2,128)} %bitcast.12, s32[1,32]{1,0:T(1,128)} %bitcast.13, bf16[256,4096]{1,0:T(8,128)(2,1)} %tokens_hbm.1, bf16[4096,1024]{1,0:T(8,128)(2,1)} %w_split_hbm.1, bf16[1024,2048]{1,0:T(8,128)(2,1)} %bitcast.9, bf16[1024,1024]{1,0:T(8,128)(2,1)} %bitcast.10, ...), custom_call_target="tpu_custom_call" | custom-call | tf_op jit(solution)/shard_map/layer/pallas_call | solution.py:574
  94.0 1.9 %copy.10 = bf16[256,1024]{1,0:T(8,128)(2,1)} copy(bf16[256,1024]{1,0:T(8,128)(2,1)} %layer.1) | data formatting | bytes 1048576
